TPU v7x, 32 devices: a whole 2x2x4 slice. The times are simulated.
32 devices in a mesh: dp: 8 (over z, x), tensor: 4 (over y, core).
Axes of the slice: x: 2, y: 2, z: 4, core: 2. Of those that a mesh axis runs over, the one named last changes fastest.
Arguments:
- inputs: bfloat16 [2, 2048, 1280], P(None, 'dp'), may hold values from -6 to 6
- cotangent: bfloat16 [2, 2048, 1280], P(None, 'dp'), may hold values from -0.625 to 0.625
- w_in: bfloat16 [1280, 5120], P('dp', 'tensor'), may hold values from -0.15625 to 0.15625
- w_out: bfloat16 [1280, 5120], P('dp', 'tensor'), may hold values from -0.078125 to 0.078125
- grad_in: float32 [1280, 5120], P('dp', 'tensor'), may hold values from -24 to 24
- grad_out: float32 [1280, 5120], P('dp', 'tensor'), may hold values from -24 to 24
Outputs:
- branch_output: bfloat16 [2, 2048, 1280], P(None, 'dp', 'tensor')
- ascent_in: float32 [1280, 5120], P('dp', 'tensor')
- ascent_out: float32 [1280, 5120], P('dp', 'tensor')
- new_grad_in: float32 [1280, 5120], P('dp', 'tensor')
- new_grad_out: float32 [1280, 5120], P('dp', 'tensor')
All inputs are finite; a program needn't handle non-finite values.
Results may differ from a plain program's by a relative error of at most 0.0064.
Values may be sent and summed in bfloat16 or wider, within the bound.
A program may use at most 128 MiB of HBM per device.

v0:
```python
import math

import jax
import jax.numpy as jnp
from jax import lax
from jax.sharding import PartitionSpec as P

D = 1280
FF = 5120


RHO = 0.1
ETA = 0.01


def gelu_parts(pre):
    cdf = 0.5 * (1.0 + lax.erf(pre * 0.7071067811865476))
    dens = jnp.exp(-0.5 * pre * pre) * 0.3989422804014327
    return (pre * cdf, cdf + pre * dens)


def token_product(left, right):
    return lax.dot_general(
        left, right, (((0,), (0,)), ((), ())), preferred_element_type=jnp.float32
    )


def local(inputs, cotangent, w_in, w_out, grad_in, grad_out):
    scale_in = jnp.abs(w_in.astype(jnp.float32)) + ETA
    scale_out = jnp.abs(w_out.astype(jnp.float32)) + ETA
    scaled_in = scale_in * grad_in
    scaled_out = scale_out * grad_out
    partial_sq = jnp.sum(scaled_in * scaled_in) + jnp.sum(scaled_out * scaled_out)
    row_total = lax.psum(partial_sq, "tensor")
    total = lax.psum(row_total, "dp")
    factor = math.sqrt(2.0 * D * FF) / jnp.sqrt(total + 1.0)
    ascent_in = factor * scaled_in
    ascent_out = factor * scaled_out
    moved_in = (w_in.astype(jnp.float32) + RHO * scale_in * ascent_in).astype(jnp.bfloat16)
    moved_out = (w_out.astype(jnp.float32) + RHO * scale_out * ascent_out).astype(jnp.bfloat16)
    micro = inputs.shape[0]
    full_in, full_out = (
        lax.all_gather(moved_in, "dp", axis=0, tiled=True),
        lax.all_gather(moved_out, "dp", axis=0, tiled=True),
    )
    outputs = []
    acts = []
    deltas = []
    for index in range(micro):
        rows = inputs[index]
        grads_y = cotangent[index]
        pre = jnp.dot(rows, full_in, preferred_element_type=jnp.float32)
        act, slope = gelu_parts(pre)
        act = act.astype(jnp.bfloat16)
        partial_y = lax.dot_general(
            act, full_out, (((1,), (1,)), ((), ())), preferred_element_type=jnp.float32
        )
        shared_y = lax.psum_scatter(partial_y, "tensor", scatter_dimension=1, tiled=True)
        outputs.append(shared_y.astype(jnp.bfloat16))
        back = jnp.dot(grads_y, full_out, preferred_element_type=jnp.float32)
        acts.append(act)
        deltas.append((back * slope).astype(jnp.bfloat16))
    branch_output = jnp.stack(outputs)
    flat_x = inputs.reshape(-1, inputs.shape[2])
    flat_dy = cotangent.reshape(-1, cotangent.shape[2])
    flat_delta = jnp.concatenate(deltas, axis=0)
    flat_act = jnp.concatenate(acts, axis=0)
    whole_in = token_product(flat_x, flat_delta)
    whole_out = token_product(flat_dy, flat_act)
    new_in, new_out = (
        lax.psum_scatter(whole_in, "dp", scatter_dimension=0, tiled=True),
        lax.psum_scatter(whole_out, "dp", scatter_dimension=0, tiled=True),
    )
    return (branch_output, ascent_in, ascent_out, new_in, new_out)


def solution(mesh):
    return jax.shard_map(
        local,
        mesh=mesh,
        in_specs=(
            P(None, "dp", None),
            P(None, "dp", None),
            P("dp", "tensor"),
            P("dp", "tensor"),
            P("dp", "tensor"),
            P("dp", "tensor"),
        ),
        out_specs=(
            P(None, "dp", "tensor"),
            P("dp", "tensor"),
            P("dp", "tensor"),
            P("dp", "tensor"),
            P("dp", "tensor"),
        ),
        check_vma=False,
    )
```

profile of v0, /device:TPU:0, one launch (start us, length us, event | category | flops | bytes accessed | tf_op | source)
XLA Modules:
  0.0 481.0 jit_solution(9765077952277714172)
XLA Ops:
  7.2 2.6 multiply_reduce_fusion
  11.2 8.9 %psum.14 = f32[]{:T(128)} all-reduce(f32[]{:T(128)S(6)} %add.44), channel_id=1, replica_groups=mesh['dp'=8,'tensor'=4] {'tensor'}, use_global_device_ids=true, to_apply=%region_2.0 | all-reduce | flops 1 | bytes 8 | tf_op jit(solution)/shard_map/psum | solution.py:34
  20.1 22.3 %psum.15 = f32[]{:T(128)} all-reduce(f32[]{:T(128)} %psum.14), channel_id=1, replica_groups=mesh['dp'=8,'tensor'=4] {'dp'}, use_global_device_ids=true, to_apply=%region_3.0 | all-reduce | flops 1 | bytes 8 | tf_op jit(solution)/shard_map/psum | solution.py:35
  43.1 1.2 fusion.22
  44.6 1.2 fusion.27
  45.9 56.3 %all-gather.3.cloned.1.call-done = bf16[1280,1280]{1,0:T(8,128)(2,1)} async-done(((bf16[160,1280]{1,0:T(8,128)(2,1)}), bf16[1280,1280]{1,0:T(8,128)(2,1)}) %all-gather.3.cloned.1.call-update) | async-done | bytes 3276816 | tf_op jit(solution)/shard_map/all_gather | solution.py:43
  102.2 4.2 multiply_convert_fusion
  106.4 58.7 %all-gather.5.cloned.1.call-done = bf16[1280,1280]{1,0:T(8,128)(2,1)} async-done(((bf16[160,1280]{1,0:T(8,128)(2,1)}), bf16[1280,1280]{1,0:T(8,128)(2,1)}) %all-gather.5.cloned.1.call-update) | async-done | bytes 3276816 | tf_op jit(solution)/shard_map/all_gather | solution.py:44
  165.1 4.1 fusion.43
  169.2 4.4 multiply_convert_fusion.1
  173.6 0.8 copy-done.8
  174.5 2.1 fusion.42
  176.7 6.4 %convolution_bitcast_fusion = f32[1280,1280]{0,1:T(8,128)} fusion(bf16[512,1280]{1,0:T(8,128)(2,1)} %bitcast.54, bf16[256,1280]{1,0:T(8,128)(2,1)} %copy-done.7, bf16[256,1280]{1,0:T(8,128)(2,1)} %copy-done.8), kind=kOutput, calls=%fused_computation | convolution fusion | flops 1680343040 | bytes 9175040 | tf_op jit(solution)/shard_map/dot_general | solution.py:23
  183.0 8.2 %copy.17 = f32[1280,1280]{1,0:T(8,128)} copy(f32[1280,1280]{0,1:T(8,128)} %convolution_bitcast_fusion) | data formatting | bytes 13107200
  191.4 2.8 fusion.3
  194.2 1.1 fusion.2
  195.5 4.6 convolution_bitcast_fusion.1
  200.1 8.3 %copy.15 = f32[1280,1280]{1,0:T(8,128)} copy(f32[1280,1280]{0,1:T(8,128)} %convolution_bitcast_fusion.1) | data formatting | bytes 13107200
  208.4 1.0 convert_bitcast_fusion
  209.4 13.9 %reduce-scatter.9.cloned.1.call-done = f32[256,320]{0,1:T(8,128)} async-done(((f32[256,1280]{0,1:T(8,128)}), f32[256,320]{0,1:T(8,128)}) %reduce-scatter.9.cloned.1.call-update) | async-done | bytes 327696 | tf_op jit(solution)/shard_map/reduce_scatter | solution.py:58
  223.3 1.0 convert_bitcast_fusion.1
  224.3 0.8 pad_maximum_fusion
  225.0 124.1 %reduce-scatter.15.cloned.1.call-done = f32[160,1280]{1,0:T(8,128)} async-done(((f32[1280,1280]{1,0:T(8,128)}), f32[160,1280]{1,0:T(8,128)}) %reduce-scatter.15.cloned.1.call-update) | async-done | bytes 819216
  349.1 125.1 %reduce-scatter.13.cloned.1.call-done = f32[160,1280]{1,0:T(8,128)} async-done(((f32[1280,1280]{1,0:T(8,128)}), f32[160,1280]{1,0:T(8,128)}) %reduce-scatter.13.cloned.1.call-update) | async-done | bytes 819216
  (32 shorter events, 0.7 us)
Async XLA Ops:
  7.2 35.9 %copy-start = (f32[160,1280]{1,0:T(8,128)S(1)}, f32[160,1280]{1,0:T(8,128)}, u32[]{:S(2)}) copy-start(f32[160,1280]{1,0:T(8,128)} %param.10) | copy-start | bytes 2457604
  7.2 35.9 %copy-start.2 = (bf16[160,1280]{1,0:T(8,128)(2,1)S(1)}, bf16[160,1280]{1,0:T(8,128)(2,1)}, u32[]{:S(2)}) copy-start(bf16[160,1280]{1,0:T(8,128)(2,1)} %param.8) | copy-start | bytes 1228804
  7.2 95.0 %all-gather.3.cloned.1.call-start = ((), (), s32[]{:S(2)}) async-start(), calls=%async_computation.4 | async-start | bytes 3686400 | tf_op jit(solution)/shard_map/all_gather | solution.py:43
  43.0 1.4 copy-start.1
  43.1 1.5 copy-start.3
  44.3 120.8 %all-gather.5.cloned.1.call-start = ((), (), s32[]{:S(2)}) async-start(), calls=%async_computation.5 | async-start | bytes 3686400 | tf_op jit(solution)/shard_map/all_gather | solution.py:44
  45.8 162.6 %reduce-scatter.11.cloned.1.call-start = ((), (), s32[]{:S(2)}) async-start(), calls=%async_computation.7 | async-start | bytes 1638400 | tf_op jit(solution)/shard_map/reduce_scatter | solution.py:58
  106.4 62.8 %copy-start.7 = (bf16[256,1280]{1,0:T(8,128)(2,1)}, bf16[256,1280]{1,0:T(8,128)(2,1)S(1)}, u32[]{:S(2)}) copy-start(bf16[256,1280]{1,0:T(8,128)(2,1)S(1)} %get-tuple-element.19) | copy-start | bytes 1966084
  169.2 5.3 %copy-start.4 = (bf16[1280,1280]{1,0:T(8,128)(2,1)S(1)}, bf16[1280,1280]{1,0:T(8,128)(2,1)}, u32[]{:S(2)}) copy-start(bf16[1280,1280]{1,0:T(8,128)(2,1)} %all-gather.5.cloned.1.call-done) | copy-start | bytes 9830404
  169.2 54.1 %reduce-scatter.9.cloned.1.call-start = ((), (), s32[]{:S(2)}) async-start(), calls=%async_computation.6 | async-start | bytes 1638400 | tf_op jit(solution)/shard_map/reduce_scatter | solution.py:58
  173.6 0.8 copy-start.8
  176.6 172.5 %reduce-scatter.15.cloned.1.call-start = ((), (), s32[]{:S(2)}) async-start(), calls=%async_computation.9 | async-start | bytes 7372800
  191.3 282.8 %reduce-scatter.13.cloned.1.call-start = ((), (), s32[]{:S(2)}) async-start(), calls=%async_computation.8 | async-start | bytes 7372800
  191.3 2.8 copy-start.5
  191.4 2.8 copy-start.9
  194.2 1.3 copy-start.6
Sparse Core Ops, SparseCore 0:
  44.5 57.6 all-gather.2
  104.9 60.1 all-gather.4
  169.3 25.0 reduce-scatter.10
  196.8 26.3 reduce-scatter.8
  227.3 121.7 reduce-scatter.14
  353.1 120.9 reduce-scatter.12
where the time goes:
time: 482 us; the launch traced here: 481 us
  waiting for transfers between devices  378 us (78%)
  blocking collectives  31.2 us (6%)
  matrix products  29.7 us (6%)
  local copies, waits for them, and re-layouts  17.7 us (4%)
  between operations  16.2 us (3%)
  other arithmetic  7.87 us (2%)
    unnamed x8, waiting for transfers between devices  249 us
    all_gather x1, waiting for transfers between devices, local(): lax.all_gather(moved_out, 'dp', axis=0, tiled=True)  58.7 us
    all_gather x1, waiting for transfers between devices, local(): lax.all_gather(moved_in, 'dp', axis=0, tiled=True)  56.3 us
    psum x1, blocking collectives, local(): total = lax.psum(row_total, 'dp')  22.3 us
    unnamed x22, local copies, waits for them, and re-layouts  17.7 us
    reduce_scatter x2, waiting for transfers between devices, local(): lax.psum_scatter(partial_y, 'tensor', scatter_dimension=1, tiled=True)  13.9 us
    dot_general x2, matrix products, token_product(): lax.dot_general(left, right, (((0,), (0,)), ((), ())), preferred_element_...  11 us
  transfers between devices with their start and end apart: 6, of which 5 were waited for; matrix products, arithmetic and copies ran while one was open for 10% of the time, Pallas kernels for 0%

commit v1 on v0

--- a/solution.py
+++ b/solution.py
@@ -1,8 +1,11 @@
+import functools
 import math
 
 import jax
 import jax.numpy as jnp
 from jax import lax
+from jax.experimental import pallas as pl
+from jax.experimental.pallas import tpu as pltpu
 from jax.sharding import PartitionSpec as P
 
 D = 1280
@@ -74,9 +77,275 @@
     return (branch_output, ascent_in, ascent_out, new_in, new_out)
 
 
+MESH = pl.DeviceIdType.MESH
+GROUP = 4
+
+
+def remote(src, dst, send, recv, where):
+    copy = pltpu.make_async_remote_copy(
+        src_ref=src, dst_ref=dst, send_sem=send, recv_sem=recv,
+        device_id=where, device_id_type=MESH,
+    )
+    copy.start()
+    return copy
+
+
+def spread_kernel(dp, tp, const, pw, pc, sq, tok, wbuf, tbuf, tot,
+                  sb1, sb2, mid, mv, s1, r1, s2, r2, ws, wr, ts, tr, ys, yr, cs, cr, loc):
+    d = lax.axis_index("dp")
+    t = lax.axis_index("tensor")
+    g = lax.rem(d, GROUP)
+    base = d - g
+    copies = [
+        remote(sq, sb1.at[k - 1], s1.at[k - 1], r1.at[k - 1], (d, lax.rem(t + k, tp)))
+        for k in range(1, tp)
+    ]
+    own_tok = pltpu.make_async_copy(tok, tbuf.at[:, g], loc.at[0])
+    own_tok.start()
+    for copy in copies:
+        copy.wait()
+    part = sq[...]
+    for k in range(tp - 1):
+        part = part + sb1[k]
+    mid[...] = part
+    copies = [
+        remote(mid, sb2.at[k - 1], s2.at[k - 1], r2.at[k - 1], (lax.rem(d + k, dp), t))
+        for k in range(1, dp)
+    ]
+    for copy in copies:
+        copy.wait()
+    for k in range(dp - 1):
+        part = part + sb2[k]
+    tot[...] = part
+    factor = const / jnp.sqrt(part[0:1, 0:1] + 1.0)
+    for j in range(GROUP):
+        mv[j] = (pw[j].astype(jnp.float32) + factor * pc[j]).astype(jnp.bfloat16)
+    own_w = pltpu.make_async_copy(mv.at[g], wbuf.at[d], loc.at[1])
+    own_w.start()
+    order = sorted(range(1, dp), key=lambda k: abs(2 * k - dp))
+    weights = []
+
+    def send_weight(k):
+        e = lax.rem(d + k, dp)
+        weights.append(remote(mv.at[lax.rem(e, GROUP)], wbuf.at[d],
+                              ws.at[k - 1], wr.at[k - 1], (e, t)))
+
+    for k in order[:3]:
+        send_weight(k)
+    tokens = []
+    for k in range(1, GROUP):
+        p = lax.rem(g + k, GROUP)
+        tokens.append(remote(tok.at[:, t], tbuf.at[:, g, t],
+                             ts.at[k - 1], tr.at[k - 1], (base + p, t)))
+    for k in order[3:]:
+        send_weight(k)
+    ty = lax.rem(t + tp // 2, tp)
+    tc = t + 1 - 2 * lax.rem(t, 2)
+    across = []
+    beside = []
+    for k in range(1, GROUP):
+        q = lax.rem(g + GROUP - k, GROUP)
+        tokens[k - 1].wait_recv()
+        piece = tbuf.at[:, q, t]
+        across.append(remote(piece, piece, ys.at[k - 1], yr.at[k - 1], (d, ty)))
+        beside.append(remote(piece, piece, cs.at[k - 1], cr.at[k - 1], (d, tc)))
+    for k in range(1, GROUP):
+        q = lax.rem(g + GROUP - k, GROUP)
+        across[k - 1].wait_recv()
+        piece = tbuf.at[:, q, ty]
+        beside.append(remote(piece, piece, cs.at[GROUP + k - 2], cr.at[GROUP + k - 2], (d, tc)))
+    for copy in tokens + across:
+        copy.wait_send()
+    for copy in weights + beside:
+        copy.wait()
+    own_tok.wait()
+    own_w.wait()
+
+
+def spread(pw, pc, sq, tok, dp, tp, const):
+    dma = lambda n: pltpu.SemaphoreType.DMA((n,))
+    vm = pl.BlockSpec(memory_space=pltpu.VMEM)
+    group, rows, cols = pw.shape
+    return pl.pallas_call(
+        functools.partial(spread_kernel, dp, tp, const),
+        out_shape=(
+            jax.ShapeDtypeStruct((dp, rows, cols), jnp.bfloat16),
+            jax.ShapeDtypeStruct((tok.shape[0], group) + tok.shape[1:], jnp.bfloat16),
+            jax.ShapeDtypeStruct((8, 128), jnp.float32),
+        ),
+        in_specs=[vm] * 4,
+        out_specs=(vm, vm, vm),
+        scratch_shapes=[
+            pltpu.VMEM((tp - 1, 8, 128), jnp.float32),
+            pltpu.VMEM((dp - 1, 8, 128), jnp.float32),
+            pltpu.VMEM((8, 128), jnp.float32),
+            pltpu.VMEM(pw.shape, jnp.bfloat16),
+            dma(tp - 1), dma(tp - 1), dma(dp - 1), dma(dp - 1), dma(dp - 1), dma(dp - 1),
+            dma(group - 1), dma(group - 1), dma(group - 1), dma(group - 1),
+            dma(2 * group - 2), dma(2 * group - 2), dma(2),
+        ],
+        compiler_params=pltpu.CompilerParams(has_side_effects=True),
+        name="spread",
+    )(pw, pc, sq, tok)
+
+
+def collect_kernel(dp, tp, pk, yt, grads, out,
+                   gbuf, cb, yst, yb, z3, zb, gs, gr, cs, cr, ys, yr, zs, zr):
+    d = lax.axis_index("dp")
+    t = lax.axis_index("tensor")
+    g = lax.rem(d, GROUP)
+    base = d - g
+    ty = lax.rem(t + tp // 2, tp)
+    tc = t + 1 - 2 * lax.rem(t, 2)
+    tcy = lax.rem(tc + tp // 2, tp)
+    depth, width = yst.shape
+    share = width // GROUP
+    step = 32
+    beside = [
+        remote(yt.at[tcy], cb.at[1], cs.at[1], cr.at[1], (d, tc)),
+        remote(yt.at[tc], cb.at[0], cs.at[0], cr.at[0], (d, tc)),
+    ]
+    sends = []
+    for k in sorted(range(1, dp), key=lambda k: abs(2 * k - dp)):
+        e = lax.rem(d + k, dp)
+        sends.append(remote(pk.at[e], gbuf.at[k - 1], gs.at[k - 1], gr.at[k - 1], (e, t)))
+    f32 = jnp.float32
+    beside[0].wait()
+
+    @pl.loop(0, depth // step)
+    def _(i):
+        at = pl.ds(pl.multiple_of(i * step, step), step)
+        yst[at, :] = (yt[ty, at, :].astype(f32) + cb[1, at, :].astype(f32)).astype(jnp.bfloat16)
+
+    across = remote(yst, yb, ys, yr, (d, ty))
+    beside[1].wait()
+    across.wait()
+
+    @pl.loop(0, depth // step)
+    def _(i):
+        at = pl.ds(pl.multiple_of(i * step, step), step)
+        whole = yt[t, at, :].astype(f32) + cb[0, at, :].astype(f32) + yb[at, :].astype(f32)
+        for p in range(GROUP):
+            z3[p, at, :] = whole[:, p * share:(p + 1) * share].astype(jnp.bfloat16)
+
+    last = []
+    for k in range(1, GROUP):
+        p = lax.rem(g + k, GROUP)
+        last.append(remote(z3.at[p], zb.at[k - 1], zs.at[k - 1], zr.at[k - 1], (base + p, t)))
+    for copy in sends:
+        copy.wait()
+    for j in range(GROUP):
+        total = None
+        for k in range(j, dp, GROUP):
+            piece = pk[d] if k == 0 else gbuf[k - 1]
+            piece = piece.astype(f32)
+            total = piece if total is None else total + piece
+        grads[lax.rem(g + GROUP - j, GROUP)] = total
+    for copy in last:
+        copy.wait()
+
+    @pl.loop(0, depth // step)
+    def _(i):
+        at = pl.ds(pl.multiple_of(i * step, step), step)
+        whole = z3[g, at, :].astype(f32)
+        for k in range(GROUP - 1):
+            whole = whole + zb[k, at, :].astype(f32)
+        out[at, :] = whole.astype(jnp.bfloat16)
+
+
+def collect(pk, yt, dp, tp):
+    dma = lambda n: pltpu.SemaphoreType.DMA((n,))
+    vm = pl.BlockSpec(memory_space=pltpu.VMEM)
+    _, rows, cols = pk.shape
+    _, depth, width = yt.shape
+    share = width // GROUP
+    bf = jnp.bfloat16
+    return pl.pallas_call(
+        functools.partial(collect_kernel, dp, tp),
+        out_shape=(
+            jax.ShapeDtypeStruct((GROUP, rows, cols), jnp.float32),
+            jax.ShapeDtypeStruct((depth, share), bf),
+        ),
+        in_specs=[vm] * 2,
+        out_specs=(vm, vm),
+        scratch_shapes=[
+            pltpu.VMEM((dp - 1, rows, cols), bf),
+            pltpu.VMEM((2, depth, width), bf),
+            pltpu.VMEM((depth, width), bf),
+            pltpu.VMEM((depth, width), bf),
+            pltpu.VMEM((GROUP, depth, share), bf),
+            pltpu.VMEM((GROUP - 1, depth, share), bf),
+            dma(dp - 1), dma(dp - 1), dma(2), dma(2),
+            pltpu.SemaphoreType.DMA, pltpu.SemaphoreType.DMA,
+            dma(GROUP - 1), dma(GROUP - 1),
+        ],
+        compiler_params=pltpu.CompilerParams(has_side_effects=True),
+        name="collect",
+    )(pk, yt)
+
+
+def regrouped(dp, tp, inputs, cotangent, w_in, w_out, grad_in, grad_out):
+    f32, bf = jnp.float32, jnp.bfloat16
+    micro, toks, width = inputs.shape
+    rows, hidden = w_in.shape
+    part = hidden // GROUP
+    scale_in = jnp.abs(w_in.astype(f32)) + ETA
+    scale_out = jnp.abs(w_out.astype(f32)) + ETA
+    scaled_in = scale_in * grad_in
+    scaled_out = scale_out * grad_out
+    partial_sq = jnp.sum(scaled_in * scaled_in) + jnp.sum(scaled_out * scaled_out)
+
+    def pack(a, b):
+        a = a.reshape(rows, GROUP, part)
+        b = b.reshape(rows, GROUP, part)
+        return jnp.concatenate([a, b], axis=2).transpose(1, 0, 2)
+
+    pw = pack(w_in, w_out)
+    pc = pack(RHO * scale_in * scaled_in, RHO * scale_out * scaled_out)
+    count = micro * toks
+    tok = jnp.stack([inputs.reshape(tp, count // tp, width), cotangent.reshape(tp, count // tp, width)])
+    const = math.sqrt(2.0 * rows * dp * hidden * tp)
+    wbuf, tbuf, tot = spread(pw, pc, jnp.full((8, 128), partial_sq, f32), tok, dp, tp, const)
+    factor = const / jnp.sqrt(tot[0, 0] + 1.0)
+    ascent_in = factor * scaled_in
+    ascent_out = factor * scaled_out
+    full = wbuf.reshape(rows * dp, 2 * part)
+    full_in, full_out = full[:, :part], full[:, part:]
+    flat_x = tbuf[0].reshape(GROUP * count, width)
+    flat_dy = tbuf[1].reshape(GROUP * count, width)
+    pre = jnp.dot(flat_x, full_in, preferred_element_type=f32)
+    act, slope = gelu_parts(pre)
+    act = act.astype(bf)
+    yt = lax.dot_general(full_out, act, (((1,), (1,)), ((), ())), preferred_element_type=f32)
+    yt = yt.astype(bf).reshape(tp, width // tp, GROUP * count)
+    back = jnp.dot(flat_dy, full_out, preferred_element_type=f32)
+    delta = (back * slope).astype(bf)
+    packed = jnp.concatenate(
+        [token_product(flat_x, delta), token_product(flat_dy, act)], axis=1
+    ).astype(bf).reshape(dp, rows, 2 * part)
+    grads, out = collect(packed, yt, dp, tp)
+    branch = out.T.reshape(micro, toks, width // tp)
+    new_in = grads[:, :, :part].transpose(1, 0, 2).reshape(rows, hidden)
+    new_out = grads[:, :, part:].transpose(1, 0, 2).reshape(rows, hidden)
+    return (branch, ascent_in, ascent_out, new_in, new_out)
+
+
+def body(dp, tp, inputs, cotangent, w_in, *rest):
+    micro, toks, width = inputs.shape
+    rows, hidden = w_in.shape
+    fits = (
+        tp == 4 and dp % GROUP == 0 and rows % 16 == 0
+        and hidden % (64 * GROUP) == 0 and (micro * toks) % 128 == 0
+        and width % (32 * tp) == 0
+    )
+    if fits:
+        return regrouped(dp, tp, inputs, cotangent, w_in, *rest)
+    return local(inputs, cotangent, w_in, *rest)
+
+
 def solution(mesh):
     return jax.shard_map(
-        local,
+        functools.partial(body, mesh.shape["dp"], mesh.shape["tensor"]),
         mesh=mesh,
         in_specs=(
             P(None, "dp", None),

time: 482 us -> 240 us (0.50)
  waiting for transfers between devices: 378 us -> 0 us
  Pallas kernels: 0 us -> 159 us
  blocking collectives: 31.2 us -> 0 us
  local copies, waits for them, and re-layouts: 17.7 us -> 37.1 us
  between operations: 16.2 us -> 2.8 us
  other arithmetic: 7.87 us -> 12.7 us
    unnamed x8 -> x0, waiting for transfers between devices: 249 us -> none
    pallas_call x0 -> x2, Pallas kernels: none -> 159 us  [the longest x1 96.9 us: spread(): pl.pallas_call(functools.partial(spread_kernel, dp, tp, const), out_shape...]
    all_gather x2 -> x0, waiting for transfers between devices: 115 us -> none  [the longest x1 58.7 us: local(): lax.all_gather(moved_out, 'dp', axis=0, tiled=True)]
    psum x2 -> x0, blocking collectives: 31.2 us -> none  [the longest x1 22.3 us: local(): total = lax.psum(row_total, 'dp')]
    unnamed x22 -> x16, local copies, waits for them, and re-layouts: 17.7 us -> 0.62 us
    dot_general x0 -> x2, local copies, waits for them, and re-layouts: none -> 15.9 us  [token_product(): lax.dot_general(left, right, (((0,), (0,)), ((), ())), preferred_element_...]
    reduce_scatter x2 -> x0, waiting for transfers between devices: 13.9 us -> none  [local(): lax.psum_scatter(partial_y, 'tensor', scatter_dimension=1, tiled=True)]
    slice x0 -> x2, local copies, waits for them, and re-layouts: none -> 10.4 us  [the longest x1 9.22 us: regrouped(): flat_x = tbuf[0].reshape(GROUP * count, width)]
  transfers between devices with their start and end apart: 6 -> 0, of which waited for: 5 -> 0; matrix products, arithmetic and copies ran while one was open for 10% -> 0% of each run, Pallas kernels for 0% -> 0%
where the time goes in v1:
time: 240 us; the launch traced here: 239 us
  Pallas kernels  159 us (66%)
  local copies, waits for them, and re-layouts  37.1 us (15%)
  matrix products  27.1 us (11%)
  other arithmetic  12.7 us (5%)
  between operations  2.8 us (1%)
    pallas_call x1, Pallas kernels, spread(): pl.pallas_call(functools.partial(spread_kernel, dp, tp, const), out_shape...  96.9 us
    pallas_call x1, Pallas kernels, collect(): pl.pallas_call(functools.partial(collect_kernel, dp, tp), out_shape=(jax....  62.6 us
    dot_general x2, local copies, waits for them, and re-layouts, token_product(): lax.dot_general(left, right, (((0,), (0,)), ((), ())), preferred_element_...  15.9 us
    dot_general x2, matrix products, token_product(): lax.dot_general(left, right, (((0,), (0,)), ((), ())), preferred_element_...  15.9 us
    slice x1, local copies, waits for them, and re-layouts, regrouped(): flat_x = tbuf[0].reshape(GROUP * count, width)  9.22 us
    dot_general x1, matrix products, regrouped(): pre = jnp.dot(flat_x, full_in, preferred_element_type=f32)  6.53 us

profile of v1, /device:TPU:0, one launch (start us, length us, event | category | flops | bytes accessed | tf_op | source)
XLA Modules:
  0.0 239.2 jit_solution(15703148913703756539)
XLA Ops:
  0.6 2.7 %multiply_reduce_fusion = (f32[]{:T(128)}, f32[160,1280]{1,0:T(8,128)S(1)}, f32[160,1280]{1,0:T(8,128)S(1)}, f32[]{:T(128)}) fusion(f32[160,1280]{1,0:T(8,128)} %param.11, bf16[160,1280]{1,0:T(8,128)(2,1)} %param.9, f32[160,1280]{1,0:T(8,128)} %param.10, bf16[160,1280]{1,0:T(8,128)(2,1)} %param.8), kind=kLoop, calls=%fused_computation.24 | loop fusion | flops 3276798 | bytes 4096008 | tf_op jit(solution)/shard_map/reduce_sum | solution.py:296
  3.3 0.7 reshape.49
  4.0 0.7 reshape.50
  4.8 1.5 maximum_bitcast_fusion.pc
  9.5 1.2 maximum_bitcast_fusion.1.pw
  10.7 3.5 %pad_maximum_fusion.tok = bf16[2,4,128,1280]{3,2,1,0:T(8,128)(2,1)} fusion(bf16[1,4,128,1280]{3,2,1,0:T(8,128)(2,1)} %bitcast.45, bf16[1,4,128,1280]{3,2,1,0:T(8,128)(2,1)} %bitcast.46), kind=kLoop, calls=%fused_computation.8 | loop fusion | flops 1310720 | bytes 5242880 | tf_op jit(solution)/shard_map/stack | solution.py:306
  14.1 96.9 %spread.1 = (bf16[8,160,640]{2,1,0:T(8,128)(2,1)}, bf16[2,4,4,128,1280]{4,3,2,1,0:T(8,128)(2,1)}, f32[8,128]{1,0:T(8,128)}) custom-call(bf16[4,160,640]{2,1,0:T(8,128)(2,1)} %maximum_bitcast_fusion.1.pw, f32[4,160,640]{2,1,0:T(8,128)} %maximum_bitcast_fusion.pc, f32[8,128]{1,0:T(8,128)} %broadcast_in_dim.3.sq, bf16[2,4,128,1280]{3,2,1,0:T(8,128)(2,1)} %pad_maximum_fusion.tok), custom_call_target="tpu_custom_call" | custom-call | tf_op jit(solution)/shard_map/spread/pallas_call | solution.py:169
  111.1 9.2 %fusion.17 = (bf16[1,4,4,128,1280]{4,3,2,1,0:T(8,128)(2,1)}, bf16[1,4,4,128,1280]{4,3,2,1,0:T(8,128)(2,1)}) fusion(bf16[2,4,4,128,1280]{4,3,2,1,0:T(8,128)(2,1)} %get-tuple-element.10), kind=kLoop, calls=%fused_computation.37 | loop fusion | bytes 20971520 | tf_op jit(solution)/shard_map/slice | solution.py:314
  120.3 6.5 %multiply_convert_fusion = (bf16[2048,320]{0,1:T(8,128)(2,1)}, f32[2048,320]{0,1:T(8,128)}) fusion(bf16[2048,1280]{1,0:T(8,128)(2,1)} %bitcast.40, bf16[1280,640]{1,0:T(8,128)(2,1)S(1)} %bitcast.50), kind=kOutput, calls=%fused_computation.9 | convolution fusion | flops 1680998400 | bytes 10158080 | tf_op jit(solution)/shard_map/dot_general | solution.py:316
  126.8 8.0 %copy.18 = bf16[1280,2048]{1,0:T(8,128)(2,1)} copy(bf16[1280,2048]{0,1:T(8,128)(2,1)} %bitcast.41) | data formatting | bytes 10485760 | tf_op jit(solution)/shard_map/dot_general | solution.py:26
  134.8 10.1 %convolution_convert_fusion.2 = bf16[8,160,320]{2,1,0:T(8,128)(2,1)S(1)} fusion(bf16[8,160,2048]{2,1,0:T(8,128)(2,1)} %bitcast.42, f32[2048,320]{0,1:T(8,128)} %get-tuple-element.34, bf16[2048,1280]{1,0:T(8,128)(2,1)} %bitcast.38, bf16[1280,640]{1,0:T(8,128)(2,1)} %bitcast.49), kind=kOutput, calls=%fused_computation.15 | convolution fusion | flops 3362406400 | bytes 14909440 | tf_op jit(solution)/shard_map/dot_general | solution.py:26
  144.9 8.0 %copy.19 = bf16[1280,2048]{1,0:T(8,128)(2,1)} copy(bf16[1280,2048]{0,1:T(8,128)(2,1)} %bitcast.39) | data formatting | bytes 10485760 | tf_op jit(solution)/shard_map/dot_general | solution.py:26
  152.9 5.8 %convolution_convert_fusion.1 = bf16[8,160,320]{2,1,0:T(8,128)(2,1)S(1)} fusion(bf16[8,160,2048]{2,1,0:T(8,128)(2,1)} %bitcast.43, bf16[2048,320]{0,1:T(8,128)(2,1)} %get-tuple-element.33), kind=kOutput, calls=%fused_computation.14 | convolution fusion | flops 1678131200 | bytes 7372800 | tf_op jit(solution)/shard_map/dot_general | solution.py:26
  158.7 1.8 pad_maximum_fusion.1.pk
  161.1 4.7 %convolution_convert_fusion = bf16[1280,2048]{1,0:T(8,128)(2,1)} fusion(bf16[2048,320]{0,1:T(8,128)(2,1)S(1)} %copy-done.7, bf16[1280,640]{1,0:T(8,128)(2,1)S(1)} %bitcast.51), kind=kOutput, calls=%fused_computation | convolution fusion | flops 1680343040 | bytes 7536640 | tf_op jit(solution)/shard_map/dot_general | solution.py:319
  165.8 62.6 %collect.1 = (f32[4,160,640]{2,1,0:T(8,128)}, bf16[320,512]{1,0:T(8,128)(2,1)}) custom-call(bf16[8,160,640]{2,1,0:T(8,128)(2,1)} %pad_maximum_fusion.1.pk, bf16[4,320,2048]{2,1,0:T(8,128)(2,1)} %bitcast.44), custom_call_target="tpu_custom_call" | custom-call | tf_op jit(solution)/shard_map/collect/pallas_call | solution.py:263
  228.3 1.8 slice_bitcast_fusion
  230.2 0.6 copy.20
  230.8 1.5 reshape.54
  233.0 1.5 reshape.55
  234.5 0.7 copy.25
  235.2 1.2 slice.25
  237.1 1.0 broadcast_multiply_fusion
  238.1 1.0 broadcast_multiply_fusion.1
  (24 shorter events, 3.2 us)
Async XLA Ops:
  4.7 3.5 %copy-start.1 = (bf16[160,1280]{1,0:T(8,128)(2,1)S(1)}, bf16[160,1280]{1,0:T(8,128)(2,1)}, u32[]{:S(2)}) copy-start(bf16[160,1280]{1,0:T(8,128)(2,1)} %param.8) | copy-start | bytes 1228804
  4.8 4.0 %copy-start = (bf16[160,1280]{1,0:T(8,128)(2,1)S(1)}, bf16[160,1280]{1,0:T(8,128)(2,1)}, u32[]{:S(2)}) copy-start(bf16[160,1280]{1,0:T(8,128)(2,1)} %param.9) | copy-start | bytes 1228804
  111.1 9.2 %copy-start.5 = (bf16[8,160,640]{2,1,0:T(8,128)(2,1)S(1)}, bf16[8,160,640]{2,1,0:T(8,128)(2,1)}, u32[]{:S(2)}) copy-start(bf16[8,160,640]{2,1,0:T(8,128)(2,1)} %get-tuple-element.11) | copy-start | bytes 4915204
  158.7 1.8 copy-start.6
  158.7 2.4 copy-start.7
  230.8 3.7 %copy-start.4 = (bf16[320,512]{1,0:T(8,128)(2,1)S(1)}, bf16[320,512]{1,0:T(8,128)(2,1)}, u32[]{:S(2)}) copy-start(bf16[320,512]{1,0:T(8,128)(2,1)} %get-tuple-element.12) | copy-start | bytes 983044
  233.0 4.1 %copy-start.2 = (f32[160,1280]{1,0:T(8,128)S(1)}, f32[160,1280]{1,0:T(8,128)}, u32[]{:S(2)}) copy-start(f32[160,1280]{1,0:T(8,128)} %param.11) | copy-start | bytes 2457604
  234.5 3.7 %copy-start.3 = (f32[160,1280]{1,0:T(8,128)S(1)}, f32[160,1280]{1,0:T(8,128)}, u32[]{:S(2)}) copy-start(f32[160,1280]{1,0:T(8,128)} %param.10) | copy-start | bytes 2457604

commit v2 on v1

--- a/solution.py
+++ b/solution.py
@@ -90,7 +90,7 @@
     return copy
 
 
-def spread_kernel(dp, tp, const, pw, pc, sq, tok, wbuf, tbuf, tot,
+def spread_kernel(dp, tp, const, pw, pc, sq, tx, tdy, wbuf, xbuf, dbuf, tot,
                   sb1, sb2, mid, mv, s1, r1, s2, r2, ws, wr, ts, tr, ys, yr, cs, cr, loc):
     d = lax.axis_index("dp")
     t = lax.axis_index("tensor")
@@ -100,8 +100,12 @@
         remote(sq, sb1.at[k - 1], s1.at[k - 1], r1.at[k - 1], (d, lax.rem(t + k, tp)))
         for k in range(1, tp)
     ]
-    own_tok = pltpu.make_async_copy(tok, tbuf.at[:, g], loc.at[0])
-    own_tok.start()
+    pairs = ((tx, xbuf), (tdy, dbuf))
+    own = [
+        pltpu.make_async_copy(src, buf.at[g], loc.at[i]) for i, (src, buf) in enumerate(pairs)
+    ]
+    for copy in own:
+        copy.start()
     for copy in copies:
         copy.wait()
     part = sq[...]
@@ -112,6 +116,12 @@
         remote(mid, sb2.at[k - 1], s2.at[k - 1], r2.at[k - 1], (lax.rem(d + k, dp), t))
         for k in range(1, dp)
     ]
+    tokens = []
+    for k in range(1, GROUP):
+        p = lax.rem(g + k, GROUP)
+        for i, (src, buf) in enumerate(pairs):
+            n = 2 * k - 2 + i
+            tokens.append(remote(src.at[t], buf.at[g, t], ts.at[n], tr.at[n], (base + p, t)))
     for copy in copies:
         copy.wait()
     for k in range(dp - 1):
@@ -120,7 +130,7 @@
     factor = const / jnp.sqrt(part[0:1, 0:1] + 1.0)
     for j in range(GROUP):
         mv[j] = (pw[j].astype(jnp.float32) + factor * pc[j]).astype(jnp.bfloat16)
-    own_w = pltpu.make_async_copy(mv.at[g], wbuf.at[d], loc.at[1])
+    own_w = pltpu.make_async_copy(mv.at[g], wbuf.at[d], loc.at[2])
     own_w.start()
     order = sorted(range(1, dp), key=lambda k: abs(2 * k - dp))
     weights = []
@@ -130,39 +140,34 @@
         weights.append(remote(mv.at[lax.rem(e, GROUP)], wbuf.at[d],
                               ws.at[k - 1], wr.at[k - 1], (e, t)))
 
-    for k in order[:3]:
-        send_weight(k)
-    tokens = []
-    for k in range(1, GROUP):
-        p = lax.rem(g + k, GROUP)
-        tokens.append(remote(tok.at[:, t], tbuf.at[:, g, t],
-                             ts.at[k - 1], tr.at[k - 1], (base + p, t)))
-    for k in order[3:]:
+    for k in order:
         send_weight(k)
     ty = lax.rem(t + tp // 2, tp)
     tc = t + 1 - 2 * lax.rem(t, 2)
     across = []
     beside = []
-    for k in range(1, GROUP):
-        q = lax.rem(g + GROUP - k, GROUP)
-        tokens[k - 1].wait_recv()
-        piece = tbuf.at[:, q, t]
-        across.append(remote(piece, piece, ys.at[k - 1], yr.at[k - 1], (d, ty)))
-        beside.append(remote(piece, piece, cs.at[k - 1], cr.at[k - 1], (d, tc)))
-    for k in range(1, GROUP):
-        q = lax.rem(g + GROUP - k, GROUP)
-        across[k - 1].wait_recv()
-        piece = tbuf.at[:, q, ty]
-        beside.append(remote(piece, piece, cs.at[GROUP + k - 2], cr.at[GROUP + k - 2], (d, tc)))
+    moves = 2 * GROUP - 2
+    for n in range(moves):
+        q = lax.rem(g + GROUP - (n // 2 + 1), GROUP)
+        tokens[n].wait_recv()
+        piece = pairs[n % 2][1].at[q, t]
+        across.append(remote(piece, piece, ys.at[n], yr.at[n], (d, ty)))
+        beside.append(remote(piece, piece, cs.at[n], cr.at[n], (d, tc)))
+    for n in range(moves):
+        q = lax.rem(g + GROUP - (n // 2 + 1), GROUP)
+        across[n].wait_recv()
+        piece = pairs[n % 2][1].at[q, ty]
+        beside.append(remote(piece, piece, cs.at[moves + n], cr.at[moves + n], (d, tc)))
     for copy in tokens + across:
         copy.wait_send()
     for copy in weights + beside:
         copy.wait()
-    own_tok.wait()
+    for copy in own:
+        copy.wait()
     own_w.wait()
 
 
-def spread(pw, pc, sq, tok, dp, tp, const):
+def spread(pw, pc, sq, tx, tdy, dp, tp, const):
     dma = lambda n: pltpu.SemaphoreType.DMA((n,))
     vm = pl.BlockSpec(memory_space=pltpu.VMEM)
     group, rows, cols = pw.shape
@@ -170,27 +175,28 @@
         functools.partial(spread_kernel, dp, tp, const),
         out_shape=(
             jax.ShapeDtypeStruct((dp, rows, cols), jnp.bfloat16),
-            jax.ShapeDtypeStruct((tok.shape[0], group) + tok.shape[1:], jnp.bfloat16),
+            jax.ShapeDtypeStruct((group,) + tx.shape, jnp.bfloat16),
+            jax.ShapeDtypeStruct((group,) + tdy.shape, jnp.bfloat16),
             jax.ShapeDtypeStruct((8, 128), jnp.float32),
         ),
-        in_specs=[vm] * 4,
-        out_specs=(vm, vm, vm),
+        in_specs=[vm] * 5,
+        out_specs=(vm, vm, vm, vm),
         scratch_shapes=[
             pltpu.VMEM((tp - 1, 8, 128), jnp.float32),
             pltpu.VMEM((dp - 1, 8, 128), jnp.float32),
             pltpu.VMEM((8, 128), jnp.float32),
             pltpu.VMEM(pw.shape, jnp.bfloat16),
             dma(tp - 1), dma(tp - 1), dma(dp - 1), dma(dp - 1), dma(dp - 1), dma(dp - 1),
-            dma(group - 1), dma(group - 1), dma(group - 1), dma(group - 1),
-            dma(2 * group - 2), dma(2 * group - 2), dma(2),
+            dma(2 * group - 2), dma(2 * group - 2), dma(2 * group - 2), dma(2 * group - 2),
+            dma(4 * group - 4), dma(4 * group - 4), dma(3),
         ],
         compiler_params=pltpu.CompilerParams(has_side_effects=True),
         name="spread",
-    )(pw, pc, sq, tok)
-
-
-def collect_kernel(dp, tp, pk, yt, grads, out,
-                   gbuf, cb, yst, yb, z3, zb, gs, gr, cs, cr, ys, yr, zs, zr):
+    )(pw, pc, sq, tx, tdy)
+
+
+def collect_kernel(dp, tp, pk, yt, new_in, new_out, out,
+                   gbuf, cb, yst, yb, z3, zb, gs, gr, cs, cr, ys, yr, zs, zr, loc):
     d = lax.axis_index("dp")
     t = lax.axis_index("tensor")
     g = lax.rem(d, GROUP)
@@ -208,8 +214,10 @@
     sends = []
     for k in sorted(range(1, dp), key=lambda k: abs(2 * k - dp)):
         e = lax.rem(d + k, dp)
-        sends.append(remote(pk.at[e], gbuf.at[k - 1], gs.at[k - 1], gr.at[k - 1], (e, t)))
+        sends.append(remote(pk.at[e], gbuf.at[d], gs.at[k - 1], gr.at[k - 1], (e, t)))
     f32 = jnp.float32
+    own = pltpu.make_async_copy(pk.at[d], gbuf.at[d], loc)
+    own.start()
     beside[0].wait()
 
     @pl.loop(0, depth // step)
@@ -234,13 +242,14 @@
         last.append(remote(z3.at[p], zb.at[k - 1], zs.at[k - 1], zr.at[k - 1], (base + p, t)))
     for copy in sends:
         copy.wait()
+    own.wait()
+    part = pk.shape[2] // 2
     for j in range(GROUP):
-        total = None
-        for k in range(j, dp, GROUP):
-            piece = pk[d] if k == 0 else gbuf[k - 1]
-            piece = piece.astype(f32)
-            total = piece if total is None else total + piece
-        grads[lax.rem(g + GROUP - j, GROUP)] = total
+        total = gbuf[j].astype(f32)
+        for e in range(j + GROUP, dp, GROUP):
+            total = total + gbuf[e].astype(f32)
+        new_in[:, j * part:(j + 1) * part] = total[:, :part]
+        new_out[:, j * part:(j + 1) * part] = total[:, part:]
     for copy in last:
         copy.wait()
 
@@ -263,13 +272,14 @@
     return pl.pallas_call(
         functools.partial(collect_kernel, dp, tp),
         out_shape=(
-            jax.ShapeDtypeStruct((GROUP, rows, cols), jnp.float32),
+            jax.ShapeDtypeStruct((rows, GROUP * cols // 2), jnp.float32),
+            jax.ShapeDtypeStruct((rows, GROUP * cols // 2), jnp.float32),
             jax.ShapeDtypeStruct((depth, share), bf),
         ),
         in_specs=[vm] * 2,
-        out_specs=(vm, vm),
+        out_specs=(vm, vm, vm),
         scratch_shapes=[
-            pltpu.VMEM((dp - 1, rows, cols), bf),
+            pltpu.VMEM((dp, rows, cols), bf),
             pltpu.VMEM((2, depth, width), bf),
             pltpu.VMEM((depth, width), bf),
             pltpu.VMEM((depth, width), bf),
@@ -277,7 +287,7 @@
             pltpu.VMEM((GROUP - 1, depth, share), bf),
             dma(dp - 1), dma(dp - 1), dma(2), dma(2),
             pltpu.SemaphoreType.DMA, pltpu.SemaphoreType.DMA,
-            dma(GROUP - 1), dma(GROUP - 1),
+            dma(GROUP - 1), dma(GROUP - 1), pltpu.SemaphoreType.DMA,
         ],
         compiler_params=pltpu.CompilerParams(has_side_effects=True),
         name="collect",
@@ -303,30 +313,34 @@
     pw = pack(w_in, w_out)
     pc = pack(RHO * scale_in * scaled_in, RHO * scale_out * scaled_out)
     count = micro * toks
-    tok = jnp.stack([inputs.reshape(tp, count // tp, width), cotangent.reshape(tp, count // tp, width)])
+    tx = inputs.reshape(tp, count // tp, width)
+    tdy = cotangent.reshape(tp, count // tp, width)
     const = math.sqrt(2.0 * rows * dp * hidden * tp)
-    wbuf, tbuf, tot = spread(pw, pc, jnp.full((8, 128), partial_sq, f32), tok, dp, tp, const)
+    wbuf, xbuf, dbuf, tot = spread(
+        pw, pc, jnp.full((8, 128), partial_sq, f32), tx, tdy, dp, tp, const
+    )
     factor = const / jnp.sqrt(tot[0, 0] + 1.0)
     ascent_in = factor * scaled_in
     ascent_out = factor * scaled_out
     full = wbuf.reshape(rows * dp, 2 * part)
     full_in, full_out = full[:, :part], full[:, part:]
-    flat_x = tbuf[0].reshape(GROUP * count, width)
-    flat_dy = tbuf[1].reshape(GROUP * count, width)
-    pre = jnp.dot(flat_x, full_in, preferred_element_type=f32)
-    act, slope = gelu_parts(pre)
+    flat_x = xbuf.reshape(GROUP * count, width)
+    flat_dy = dbuf.reshape(GROUP * count, width)
+
+    def against(weight, tokens):
+        return lax.dot_general(weight, tokens, (((0,), (1,)), ((), ())), preferred_element_type=f32)
+
+    act, slope = gelu_parts(against(full_in, flat_x))
     act = act.astype(bf)
-    yt = lax.dot_general(full_out, act, (((1,), (1,)), ((), ())), preferred_element_type=f32)
+    yt = jnp.dot(full_out, act, preferred_element_type=f32)
     yt = yt.astype(bf).reshape(tp, width // tp, GROUP * count)
-    back = jnp.dot(flat_dy, full_out, preferred_element_type=f32)
-    delta = (back * slope).astype(bf)
-    packed = jnp.concatenate(
-        [token_product(flat_x, delta), token_product(flat_dy, act)], axis=1
-    ).astype(bf).reshape(dp, rows, 2 * part)
-    grads, out = collect(packed, yt, dp, tp)
+    delta = (against(full_out, flat_dy) * slope).astype(bf)
+    packed = jnp.concatenate([
+        jnp.dot(delta, flat_x, preferred_element_type=f32).astype(bf),
+        jnp.dot(act, flat_dy, preferred_element_type=f32).astype(bf),
+    ], axis=0).T.reshape(dp, rows, 2 * part)
+    new_in, new_out, out = collect(packed, yt, dp, tp)
     branch = out.T.reshape(micro, toks, width // tp)
-    new_in = grads[:, :, :part].transpose(1, 0, 2).reshape(rows, hidden)
-    new_out = grads[:, :, part:].transpose(1, 0, 2).reshape(rows, hidden)
     return (branch, ascent_in, ascent_out, new_in, new_out)
 
 

time: 240 us -> 200 us (0.83)
  local copies, waits for them, and re-layouts: 37.1 us -> 10.4 us
  Pallas kernels: 159 us -> 150 us
  other arithmetic: 12.7 us -> 7.48 us
    dot_general x2 -> x0, local copies, waits for them, and re-layouts: 15.9 us -> none  [token_product(): lax.dot_general(left, right, (((0,), (0,)), ((), ())), preferred_element_...]
    pallas_call x1, Pallas kernels: 96.9 us -> 82.2 us  [spread(): pl.pallas_call(functools.partial(spread_kernel, dp, tp, const), out_shape...]
    slice x1 -> x0, local copies, waits for them, and re-layouts: 9.22 us -> none  [regrouped(): flat_x = tbuf[0].reshape(GROUP * count, width)]
    pallas_call x1, Pallas kernels: 62.6 us -> 67.7 us  [collect(): pl.pallas_call(functools.partial(collect_kernel, dp, tp), out_shape=(jax....]
    another operation x1 -> x0, other arithmetic: 3.49 us -> none  [regrouped(): jnp.stack([inputs.reshape(tp, count // tp, width), cotangent.reshape(tp,...]
    reshape x2 -> x0, local copies, waits for them, and re-layouts: 2.99 us -> none  [the longest x1 1.49 us: regrouped(): new_in = grads[:, :, :part].transpose(1, 0, 2).reshape(rows, hidden)]
where the time goes in v2:
time: 200 us
  Pallas kernels  150 us (75%)
  matrix products  29.2 us (15%)
  local copies, waits for them, and re-layouts  10.4 us (5%)
  other arithmetic  7.48 us (4%)
  between operations  2.78 us (1%)
    pallas_call x1, Pallas kernels, spread(): pl.pallas_call(functools.partial(spread_kernel, dp, tp, const), out_shape...  82.2 us
    pallas_call x1, Pallas kernels, collect(): pl.pallas_call(functools.partial(collect_kernel, dp, tp), out_shape=(jax....  67.7 us
    dot_general x1, matrix products, regrouped(): jnp.dot(delta, flat_x, preferred_element_type=f32).astype(bf)  10.2 us
    dot_general x1, matrix products, against(): lax.dot_general(weight, tokens, (((0,), (1,)), ((), ())), preferred_eleme...  7.26 us
    dot_general x1, matrix products, regrouped(): yt = jnp.dot(full_out, act, preferred_element_type=f32)  6.87 us
    dot_general x1, matrix products, regrouped(): jnp.dot(act, flat_dy, preferred_element_type=f32).astype(bf)  4.8 us

profile of v2, /device:TPU:0, one launch (start us, length us, event | category | flops | bytes accessed | tf_op | source)
XLA Modules:
  0.0 199.7 jit_solution(4028201698103506425)
XLA Ops:
  0.6 2.7 %multiply_reduce_fusion = (f32[]{:T(128)}, f32[160,1280]{1,0:T(8,128)S(1)}, f32[160,1280]{1,0:T(8,128)S(1)}, f32[]{:T(128)}) fusion(f32[160,1280]{1,0:T(8,128)} %param.11, bf16[160,1280]{1,0:T(8,128)(2,1)} %param.9, f32[160,1280]{1,0:T(8,128)} %param.10, bf16[160,1280]{1,0:T(8,128)(2,1)} %param.8), kind=kLoop, calls=%fused_computation.19 | loop fusion | flops 3276798 | bytes 4096008 | tf_op jit(solution)/shard_map/reduce_sum | solution.py:306
  3.3 0.7 reshape.53
  4.0 0.1 copy.15
  4.0 0.7 reshape.54
  4.8 0.1 copy.16
  4.8 1.5 maximum_bitcast_fusion.pc
  7.6 0.6 broadcast_in_dim.3.sq
  8.2 0.5 reshape.51
  8.9 0.5 reshape.52
  9.5 1.2 maximum_bitcast_fusion.2.pw
  10.7 82.2 %spread.1 = (bf16[8,160,640]{2,1,0:T(8,128)(2,1)}, bf16[4,4,128,1280]{3,2,1,0:T(8,128)(2,1)}, bf16[4,4,128,1280]{3,2,1,0:T(8,128)(2,1)}, f32[8,128]{1,0:T(8,128)}) custom-call(bf16[4,160,640]{2,1,0:T(8,128)(2,1)} %maximum_bitcast_fusion.2.pw, f32[4,160,640]{2,1,0:T(8,128)} %maximum_bitcast_fusion.pc, f32[8,128]{1,0:T(8,128)} %broadcast_in_dim.3.sq, ...), custom_call_target="tpu_custom_call" | custom-call | tf_op jit(solution)/shard_map/spread/pallas_call | solution.py:174
  92.9 7.3 %multiply_convert_fusion = (bf16[320,2048]{1,0:T(8,128)(2,1)}, f32[320,2048]{1,0:T(8,128)}) fusion(bf16[2048,1280]{1,0:T(8,128)(2,1)} %bitcast.33, bf16[1280,640]{1,0:T(8,128)(2,1)} %bitcast.35), kind=kOutput, calls=%fused_computation.10 | convolution fusion | flops 1680998400 | bytes 10158080 | tf_op jit(solution)/shard_map/dot_general | solution.py:331
  100.1 10.2 %convolution_convert_fusion.2 = bf16[320,1280]{1,0:T(8,128)(2,1)} fusion(bf16[2048,1280]{1,0:T(8,128)(2,1)} %bitcast.34, bf16[2048,1280]{1,0:T(8,128)(2,1)} %bitcast.31, f32[320,2048]{1,0:T(8,128)} %get-tuple-element.34, bf16[1280,640]{1,0:T(8,128)(2,1)S(1)} %bitcast.37), kind=kOutput, calls=%fused_computation.4 | convolution fusion | flops 3362406400 | bytes 14909440 | tf_op jit(solution)/shard_map/dot_general | solution.py:339
  110.4 4.8 %convolution_convert_fusion.1 = bf16[320,1280]{1,0:T(8,128)(2,1)S(1)} fusion(bf16[320,2048]{1,0:T(8,128)(2,1)} %get-tuple-element.33, bf16[2048,1280]{1,0:T(8,128)(2,1)} %bitcast.32), kind=kOutput, calls=%fused_computation.3 | convolution fusion | flops 1678131200 | bytes 7372800 | tf_op jit(solution)/shard_map/dot_general | solution.py:340
  115.2 0.1 maximum_bitcast_fusion.1
  115.3 2.3 %copy.17 = bf16[1280,640]{1,0:T(8,128)(2,1)} copy(bf16[1280,640]{0,1:T(8,128)(2,1)S(1)} %maximum_bitcast_fusion.1) | data formatting | bytes 3276800 | tf_op jit(solution)/shard_map/transpose | solution.py:341
  117.6 6.9 %convolution_convert_fusion = bf16[1280,2048]{1,0:T(8,128)(2,1)} fusion(bf16[320,2048]{1,0:T(8,128)(2,1)} %get-tuple-element.33, bf16[1280,640]{1,0:T(8,128)(2,1)} %bitcast.36), kind=kOutput, calls=%fused_computation | convolution fusion | flops 1680343040 | bytes 7536640 | tf_op jit(solution)/shard_map/dot_general | solution.py:335
  124.4 67.7 %collect.1 = (f32[160,1280]{1,0:T(8,128)}, f32[160,1280]{1,0:T(8,128)}, bf16[320,512]{1,0:T(8,128)(2,1)}) custom-call(bf16[8,160,640]{2,1,0:T(8,128)(2,1)} %bitcast.25, bf16[4,320,2048]{2,1,0:T(8,128)(2,1)} %bitcast.26), custom_call_target="tpu_custom_call" | custom-call | tf_op jit(solution)/shard_map/collect/pallas_call | solution.py:272
  192.1 1.8 copy.21
  194.0 1.2 slice.11
  195.9 1.0 broadcast_multiply_fusion
  196.9 1.0 broadcast_multiply_fusion.1
  197.9 0.9 copy.24
  198.8 0.9 copy.25
  (18 shorter events, 0.2 us)
Async XLA Ops:
  4.7 3.5 %copy-start.1 = (bf16[160,1280]{1,0:T(8,128)(2,1)S(1)}, bf16[160,1280]{1,0:T(8,128)(2,1)}, u32[]{:S(2)}) copy-start(bf16[160,1280]{1,0:T(8,128)(2,1)} %param.8) | copy-start | bytes 1228804
  4.8 4.0 %copy-start = (bf16[160,1280]{1,0:T(8,128)(2,1)S(1)}, bf16[160,1280]{1,0:T(8,128)(2,1)}, u32[]{:S(2)}) copy-start(bf16[160,1280]{1,0:T(8,128)(2,1)} %param.9) | copy-start | bytes 1228804
  92.9 7.3 %copy-start.7 = (bf16[8,160,640]{2,1,0:T(8,128)(2,1)S(1)}, bf16[8,160,640]{2,1,0:T(8,128)(2,1)}, u32[]{:S(2)}) copy-start(bf16[8,160,640]{2,1,0:T(8,128)(2,1)} %get-tuple-element.12) | copy-start | bytes 4915204
  110.4 4.8 %copy-start.6 = (bf16[320,1280]{1,0:T(8,128)(2,1)S(1)}, bf16[320,1280]{1,0:T(8,128)(2,1)}, u32[]{:S(2)}) copy-start(bf16[320,1280]{1,0:T(8,128)(2,1)} %convolution_convert_fusion.2) | copy-start | bytes 2457604
  124.4 71.4 %copy-start.2 = (f32[160,1280]{1,0:T(8,128)S(1)}, f32[160,1280]{1,0:T(8,128)}, u32[]{:S(2)}) copy-start(f32[160,1280]{1,0:T(8,128)} %param.11) | copy-start | bytes 2457604
  192.1 4.8 %copy-start.3 = (f32[160,1280]{1,0:T(8,128)S(1)}, f32[160,1280]{1,0:T(8,128)}, u32[]{:S(2)}) copy-start(f32[160,1280]{1,0:T(8,128)} %param.10) | copy-start | bytes 2457604
  192.1 5.8 %copy-start.5 = (f32[160,1280]{1,0:T(8,128)S(1)}, f32[160,1280]{1,0:T(8,128)}, u32[]{:S(2)}) copy-start(f32[160,1280]{1,0:T(8,128)} %get-tuple-element.45) | copy-start | bytes 2457604
  195.8 3.0 %copy-start.4 = (f32[160,1280]{1,0:T(8,128)S(1)}, f32[160,1280]{1,0:T(8,128)}, u32[]{:S(2)}) copy-start(f32[160,1280]{1,0:T(8,128)} %get-tuple-element.46) | copy-start | bytes 2457604

commit v3 on v2

--- a/solution.py
+++ b/solution.py
@@ -204,13 +204,17 @@
     ty = lax.rem(t + tp // 2, tp)
     tc = t + 1 - 2 * lax.rem(t, 2)
     tcy = lax.rem(tc + tp // 2, tp)
-    depth, width = yst.shape
-    share = width // GROUP
+    _, depth, share = yst.shape
     step = 32
-    beside = [
-        remote(yt.at[tcy], cb.at[1], cs.at[1], cr.at[1], (d, tc)),
-        remote(yt.at[tc], cb.at[0], cs.at[0], cr.at[0], (d, tc)),
-    ]
+    order = list(range(1, GROUP)) + [0]
+    columns = [pl.ds(pl.multiple_of(lax.rem(g + k, GROUP) * share, share), share) for k in range(GROUP)]
+    beside = [{}, {}]
+    for half, whose in ((1, tcy), (0, tc)):
+        for k in order:
+            n = half * GROUP + k
+            beside[half][k] = remote(
+                yt.at[whose, :, columns[k]], cb.at[half, k], cs.at[n], cr.at[n], (d, tc)
+            )
     sends = []
     for k in sorted(range(1, dp), key=lambda k: abs(2 * k - dp)):
         e = lax.rem(d + k, dp)
@@ -218,28 +222,31 @@
     f32 = jnp.float32
     own = pltpu.make_async_copy(pk.at[d], gbuf.at[d], loc)
     own.start()
-    beside[0].wait()
-
-    @pl.loop(0, depth // step)
-    def _(i):
-        at = pl.ds(pl.multiple_of(i * step, step), step)
-        yst[at, :] = (yt[ty, at, :].astype(f32) + cb[1, at, :].astype(f32)).astype(jnp.bfloat16)
-
-    across = remote(yst, yb, ys, yr, (d, ty))
-    beside[1].wait()
-    across.wait()
-
-    @pl.loop(0, depth // step)
-    def _(i):
-        at = pl.ds(pl.multiple_of(i * step, step), step)
-        whole = yt[t, at, :].astype(f32) + cb[0, at, :].astype(f32) + yb[at, :].astype(f32)
-        for p in range(GROUP):
-            z3[p, at, :] = whole[:, p * share:(p + 1) * share].astype(jnp.bfloat16)
-
+    across = {}
+    for k in order:
+        beside[1][k].wait()
+
+        @pl.loop(0, depth // step)
+        def _(i):
+            at = pl.ds(pl.multiple_of(i * step, step), step)
+            whole = yt[ty, at, columns[k]].astype(f32) + cb[1, k, at, :].astype(f32)
+            yst[k, at, :] = whole.astype(jnp.bfloat16)
+
+        across[k] = remote(yst.at[k], yb.at[k], ys.at[k], yr.at[k], (d, ty))
     last = []
-    for k in range(1, GROUP):
-        p = lax.rem(g + k, GROUP)
-        last.append(remote(z3.at[p], zb.at[k - 1], zs.at[k - 1], zr.at[k - 1], (base + p, t)))
+    for k in order:
+        beside[0][k].wait()
+        across[k].wait()
+
+        @pl.loop(0, depth // step)
+        def _(i):
+            at = pl.ds(pl.multiple_of(i * step, step), step)
+            whole = yt[t, at, columns[k]].astype(f32) + cb[0, k, at, :].astype(f32)
+            z3[k, at, :] = (whole + yb[k, at, :].astype(f32)).astype(jnp.bfloat16)
+
+        if k > 0:
+            p = lax.rem(g + k, GROUP)
+            last.append(remote(z3.at[k], zb.at[k - 1], zs.at[k - 1], zr.at[k - 1], (base + p, t)))
     for copy in sends:
         copy.wait()
     own.wait()
@@ -256,7 +263,7 @@
     @pl.loop(0, depth // step)
     def _(i):
         at = pl.ds(pl.multiple_of(i * step, step), step)
-        whole = z3[g, at, :].astype(f32)
+        whole = z3[0, at, :].astype(f32)
         for k in range(GROUP - 1):
             whole = whole + zb[k, at, :].astype(f32)
         out[at, :] = whole.astype(jnp.bfloat16)
@@ -280,13 +287,13 @@
         out_specs=(vm, vm, vm),
         scratch_shapes=[
             pltpu.VMEM((dp, rows, cols), bf),
-            pltpu.VMEM((2, depth, width), bf),
-            pltpu.VMEM((depth, width), bf),
-            pltpu.VMEM((depth, width), bf),
+            pltpu.VMEM((2, GROUP, depth, share), bf),
+            pltpu.VMEM((GROUP, depth, share), bf),
+            pltpu.VMEM((GROUP, depth, share), bf),
             pltpu.VMEM((GROUP, depth, share), bf),
             pltpu.VMEM((GROUP - 1, depth, share), bf),
-            dma(dp - 1), dma(dp - 1), dma(2), dma(2),
-            pltpu.SemaphoreType.DMA, pltpu.SemaphoreType.DMA,
+            dma(dp - 1), dma(dp - 1), dma(2 * GROUP), dma(2 * GROUP),
+            dma(GROUP), dma(GROUP),
             dma(GROUP - 1), dma(GROUP - 1), pltpu.SemaphoreType.DMA,
         ],
         compiler_params=pltpu.CompilerParams(has_side_effects=True),

time: 200 us -> 195 us (0.975)
  Pallas kernels: 150 us -> 144 us
    pallas_call x1, Pallas kernels: 67.7 us -> 61.8 us  [collect(): pl.pallas_call(functools.partial(collect_kernel, dp, tp), out_shape=(jax....]
where the time goes in v3:
time: 195 us; the launch traced here: 194 us
  Pallas kernels  144 us (74%)
  matrix products  29.2 us (15%)
  local copies, waits for them, and re-layouts  10.4 us (5%)
  other arithmetic  7.48 us (4%)
  between operations  2.78 us (1%)
    pallas_call x1, Pallas kernels, spread(): pl.pallas_call(functools.partial(spread_kernel, dp, tp, const), out_shape...  82.2 us
    pallas_call x1, Pallas kernels, collect(): pl.pallas_call(functools.partial(collect_kernel, dp, tp), out_shape=(jax....  61.8 us
    dot_general x1, matrix products, regrouped(): jnp.dot(delta, flat_x, preferred_element_type=f32).astype(bf)  10.2 us
    dot_general x1, matrix products, against(): lax.dot_general(weight, tokens, (((0,), (1,)), ((), ())), preferred_eleme...  7.26 us
    dot_general x1, matrix products, regrouped(): yt = jnp.dot(full_out, act, preferred_element_type=f32)  6.87 us
    dot_general x1, matrix products, regrouped(): jnp.dot(act, flat_dy, preferred_element_type=f32).astype(bf)  4.8 us

profile of v3, /device:TPU:0, one launch (start us, length us, event | category | flops | bytes accessed | tf_op | source)
XLA Modules:
  0.0 193.8 jit_solution(15714565541073714728)
XLA Ops:
  0.6 2.7 %multiply_reduce_fusion = (f32[]{:T(128)}, f32[160,1280]{1,0:T(8,128)S(1)}, f32[160,1280]{1,0:T(8,128)S(1)}, f32[]{:T(128)}) fusion(f32[160,1280]{1,0:T(8,128)} %param.11, bf16[160,1280]{1,0:T(8,128)(2,1)} %param.9, f32[160,1280]{1,0:T(8,128)} %param.10, bf16[160,1280]{1,0:T(8,128)(2,1)} %param.8), kind=kLoop, calls=%fused_computation.19 | loop fusion | flops 3276798 | bytes 4096008 | tf_op jit(solution)/shard_map/reduce_sum | solution.py:313
  3.3 0.7 reshape.53
  4.0 0.1 copy.15
  4.0 0.7 reshape.54
  4.8 0.1 copy.16
  4.8 1.5 maximum_bitcast_fusion.pc
  7.6 0.6 broadcast_in_dim.3.sq
  8.2 0.5 reshape.51
  8.9 0.5 reshape.52
  9.5 1.2 maximum_bitcast_fusion.2.pw
  10.7 82.2 %spread.1 = (bf16[8,160,640]{2,1,0:T(8,128)(2,1)}, bf16[4,4,128,1280]{3,2,1,0:T(8,128)(2,1)}, bf16[4,4,128,1280]{3,2,1,0:T(8,128)(2,1)}, f32[8,128]{1,0:T(8,128)}) custom-call(bf16[4,160,640]{2,1,0:T(8,128)(2,1)} %maximum_bitcast_fusion.2.pw, f32[4,160,640]{2,1,0:T(8,128)} %maximum_bitcast_fusion.pc, f32[8,128]{1,0:T(8,128)} %broadcast_in_dim.3.sq, ...), custom_call_target="tpu_custom_call" | custom-call | tf_op jit(solution)/shard_map/spread/pallas_call | solution.py:174
  92.9 7.3 %multiply_convert_fusion = (bf16[320,2048]{1,0:T(8,128)(2,1)}, f32[320,2048]{1,0:T(8,128)}) fusion(bf16[2048,1280]{1,0:T(8,128)(2,1)} %bitcast.33, bf16[1280,640]{1,0:T(8,128)(2,1)} %bitcast.35), kind=kOutput, calls=%fused_computation.10 | convolution fusion | flops 1680998400 | bytes 10158080 | tf_op jit(solution)/shard_map/dot_general | solution.py:338
  100.1 10.2 %convolution_convert_fusion.2 = bf16[320,1280]{1,0:T(8,128)(2,1)} fusion(bf16[2048,1280]{1,0:T(8,128)(2,1)} %bitcast.34, bf16[2048,1280]{1,0:T(8,128)(2,1)} %bitcast.31, f32[320,2048]{1,0:T(8,128)} %get-tuple-element.34, bf16[1280,640]{1,0:T(8,128)(2,1)S(1)} %bitcast.37), kind=kOutput, calls=%fused_computation.4 | convolution fusion | flops 3362406400 | bytes 14909440 | tf_op jit(solution)/shard_map/dot_general | solution.py:346
  110.4 4.8 %convolution_convert_fusion.1 = bf16[320,1280]{1,0:T(8,128)(2,1)S(1)} fusion(bf16[320,2048]{1,0:T(8,128)(2,1)} %get-tuple-element.33, bf16[2048,1280]{1,0:T(8,128)(2,1)} %bitcast.32), kind=kOutput, calls=%fused_computation.3 | convolution fusion | flops 1678131200 | bytes 7372800 | tf_op jit(solution)/shard_map/dot_general | solution.py:347
  115.2 0.1 maximum_bitcast_fusion.1
  115.3 2.3 %copy.17 = bf16[1280,640]{1,0:T(8,128)(2,1)} copy(bf16[1280,640]{0,1:T(8,128)(2,1)S(1)} %maximum_bitcast_fusion.1) | data formatting | bytes 3276800 | tf_op jit(solution)/shard_map/transpose | solution.py:348
  117.6 6.9 %convolution_convert_fusion = bf16[1280,2048]{1,0:T(8,128)(2,1)} fusion(bf16[320,2048]{1,0:T(8,128)(2,1)} %get-tuple-element.33, bf16[1280,640]{1,0:T(8,128)(2,1)} %bitcast.36), kind=kOutput, calls=%fused_computation | convolution fusion | flops 1680343040 | bytes 7536640 | tf_op jit(solution)/shard_map/dot_general | solution.py:342
  124.4 61.8 %collect.1 = (f32[160,1280]{1,0:T(8,128)}, f32[160,1280]{1,0:T(8,128)}, bf16[320,512]{1,0:T(8,128)(2,1)}) custom-call(bf16[8,160,640]{2,1,0:T(8,128)(2,1)} %bitcast.25, bf16[4,320,2048]{2,1,0:T(8,128)(2,1)} %bitcast.26), custom_call_target="tpu_custom_call" | custom-call | tf_op jit(solution)/shard_map/collect/pallas_call | solution.py:279
  186.3 1.8 copy.21
  188.1 1.2 slice.11
  190.0 1.0 broadcast_multiply_fusion
  191.0 1.0 broadcast_multiply_fusion.1
  192.1 0.9 copy.24
  192.9 0.9 copy.25
  (18 shorter events, 0.2 us)
Async XLA Ops:
  4.7 3.5 %copy-start.1 = (bf16[160,1280]{1,0:T(8,128)(2,1)S(1)}, bf16[160,1280]{1,0:T(8,128)(2,1)}, u32[]{:S(2)}) copy-start(bf16[160,1280]{1,0:T(8,128)(2,1)} %param.8) | copy-start | bytes 1228804
  4.8 4.0 %copy-start = (bf16[160,1280]{1,0:T(8,128)(2,1)S(1)}, bf16[160,1280]{1,0:T(8,128)(2,1)}, u32[]{:S(2)}) copy-start(bf16[160,1280]{1,0:T(8,128)(2,1)} %param.9) | copy-start | bytes 1228804
  92.9 7.3 %copy-start.7 = (bf16[8,160,640]{2,1,0:T(8,128)(2,1)S(1)}, bf16[8,160,640]{2,1,0:T(8,128)(2,1)}, u32[]{:S(2)}) copy-start(bf16[8,160,640]{2,1,0:T(8,128)(2,1)} %get-tuple-element.12) | copy-start | bytes 4915204
  110.4 4.8 %copy-start.6 = (bf16[320,1280]{1,0:T(8,128)(2,1)S(1)}, bf16[320,1280]{1,0:T(8,128)(2,1)}, u32[]{:S(2)}) copy-start(bf16[320,1280]{1,0:T(8,128)(2,1)} %convolution_convert_fusion.2) | copy-start | bytes 2457604
  124.4 65.5 %copy-start.2 = (f32[160,1280]{1,0:T(8,128)S(1)}, f32[160,1280]{1,0:T(8,128)}, u32[]{:S(2)}) copy-start(f32[160,1280]{1,0:T(8,128)} %param.11) | copy-start | bytes 2457604
  186.2 4.8 %copy-start.3 = (f32[160,1280]{1,0:T(8,128)S(1)}, f32[160,1280]{1,0:T(8,128)}, u32[]{:S(2)}) copy-start(f32[160,1280]{1,0:T(8,128)} %param.10) | copy-start | bytes 2457604
  186.2 5.8 %copy-start.5 = (f32[160,1280]{1,0:T(8,128)S(1)}, f32[160,1280]{1,0:T(8,128)}, u32[]{:S(2)}) copy-start(f32[160,1280]{1,0:T(8,128)} %get-tuple-element.45) | copy-start | bytes 2457604
  190.0 3.0 %copy-start.4 = (f32[160,1280]{1,0:T(8,128)S(1)}, f32[160,1280]{1,0:T(8,128)}, u32[]{:S(2)}) copy-start(f32[160,1280]{1,0:T(8,128)} %get-tuple-element.46) | copy-start | bytes 2457604

commit v4 on v3

--- a/solution.py
+++ b/solution.py
@@ -90,12 +90,18 @@
     return copy
 
 
-def spread_kernel(dp, tp, const, pw, pc, sq, tx, tdy, wbuf, xbuf, dbuf, tot,
-                  sb1, sb2, mid, mv, s1, r1, s2, r2, ws, wr, ts, tr, ys, yr, cs, cr, loc):
+def spread_kernel(dp, tp, const, wi, wo, gi, go, tx, tdy, wbuf, xbuf, dbuf, tot,
+                  sq, sb1, sb2, mid, mv, s1, r1, s2, r2, ws, wr, ts, tr, ys, yr, cs, cr, loc):
     d = lax.axis_index("dp")
     t = lax.axis_index("tensor")
     g = lax.rem(d, GROUP)
     base = d - g
+    f32 = jnp.float32
+    square = jnp.zeros((1, 1), f32)
+    for w, grad in ((wi, gi), (wo, go)):
+        scaled = (jnp.abs(w[...].astype(f32)) + ETA) * grad[...]
+        square = square + jnp.sum(scaled * scaled, axis=(0, 1), keepdims=True)
+    sq[...] = jnp.broadcast_to(square, sq.shape)
     copies = [
         remote(sq, sb1.at[k - 1], s1.at[k - 1], r1.at[k - 1], (d, lax.rem(t + k, tp)))
         for k in range(1, tp)
@@ -128,8 +134,15 @@
         part = part + sb2[k]
     tot[...] = part
     factor = const / jnp.sqrt(part[0:1, 0:1] + 1.0)
+    part_cols = wi.shape[1] // GROUP
     for j in range(GROUP):
-        mv[j] = (pw[j].astype(jnp.float32) + factor * pc[j]).astype(jnp.bfloat16)
+        for i, (w, grad) in enumerate(((wi, gi), (wo, go))):
+            weight = w[:, j * part_cols:(j + 1) * part_cols].astype(f32)
+            scale = jnp.abs(weight) + ETA
+            ascent = factor * (scale * grad[:, j * part_cols:(j + 1) * part_cols])
+            mv[j, :, i * part_cols:(i + 1) * part_cols] = (
+                weight + RHO * scale * ascent
+            ).astype(jnp.bfloat16)
     own_w = pltpu.make_async_copy(mv.at[g], wbuf.at[d], loc.at[2])
     own_w.start()
     order = sorted(range(1, dp), key=lambda k: abs(2 * k - dp))
@@ -167,10 +180,11 @@
     own_w.wait()
 
 
-def spread(pw, pc, sq, tx, tdy, dp, tp, const):
+def spread(w_in, w_out, grad_in, grad_out, tx, tdy, dp, tp, const):
     dma = lambda n: pltpu.SemaphoreType.DMA((n,))
     vm = pl.BlockSpec(memory_space=pltpu.VMEM)
-    group, rows, cols = pw.shape
+    rows, hidden = w_in.shape
+    group, cols = GROUP, 2 * hidden // GROUP
     return pl.pallas_call(
         functools.partial(spread_kernel, dp, tp, const),
         out_shape=(
@@ -179,20 +193,21 @@
             jax.ShapeDtypeStruct((group,) + tdy.shape, jnp.bfloat16),
             jax.ShapeDtypeStruct((8, 128), jnp.float32),
         ),
-        in_specs=[vm] * 5,
+        in_specs=[vm] * 6,
         out_specs=(vm, vm, vm, vm),
         scratch_shapes=[
+            pltpu.VMEM((8, 128), jnp.float32),
             pltpu.VMEM((tp - 1, 8, 128), jnp.float32),
             pltpu.VMEM((dp - 1, 8, 128), jnp.float32),
             pltpu.VMEM((8, 128), jnp.float32),
-            pltpu.VMEM(pw.shape, jnp.bfloat16),
+            pltpu.VMEM((group, rows, cols), jnp.bfloat16),
             dma(tp - 1), dma(tp - 1), dma(dp - 1), dma(dp - 1), dma(dp - 1), dma(dp - 1),
             dma(2 * group - 2), dma(2 * group - 2), dma(2 * group - 2), dma(2 * group - 2),
             dma(4 * group - 4), dma(4 * group - 4), dma(3),
         ],
         compiler_params=pltpu.CompilerParams(has_side_effects=True),
         name="spread",
-    )(pw, pc, sq, tx, tdy)
+    )(w_in, w_out, grad_in, grad_out, tx, tdy)
 
 
 def collect_kernel(dp, tp, pk, yt, new_in, new_out, out,
@@ -310,21 +325,12 @@
     scale_out = jnp.abs(w_out.astype(f32)) + ETA
     scaled_in = scale_in * grad_in
     scaled_out = scale_out * grad_out
-    partial_sq = jnp.sum(scaled_in * scaled_in) + jnp.sum(scaled_out * scaled_out)
-
-    def pack(a, b):
-        a = a.reshape(rows, GROUP, part)
-        b = b.reshape(rows, GROUP, part)
-        return jnp.concatenate([a, b], axis=2).transpose(1, 0, 2)
-
-    pw = pack(w_in, w_out)
-    pc = pack(RHO * scale_in * scaled_in, RHO * scale_out * scaled_out)
     count = micro * toks
     tx = inputs.reshape(tp, count // tp, width)
     tdy = cotangent.reshape(tp, count // tp, width)
     const = math.sqrt(2.0 * rows * dp * hidden * tp)
     wbuf, xbuf, dbuf, tot = spread(
-        pw, pc, jnp.full((8, 128), partial_sq, f32), tx, tdy, dp, tp, const
+        w_in, w_out, grad_in, grad_out, tx, tdy, dp, tp, const
     )
     factor = const / jnp.sqrt(tot[0, 0] + 1.0)
     ascent_in = factor * scaled_in

time: 195 us -> 183 us (0.938)
  other arithmetic: 7.48 us -> 1.54 us
  local copies, waits for them, and re-layouts: 10.4 us -> 7.05 us
    reshape x8 -> x0, local copies, waits for them, and re-layouts: 2.73 us -> none  [the longest x4 1.36 us: pack(): b = b.reshape(rows, GROUP, part)]
    transpose x2 -> x0, other arithmetic: 2.66 us -> none  [pack(): return jnp.concatenate([a, b], axis=2).transpose(1, 0, 2)]
    reduce_sum x1 -> x0, other arithmetic: 2.65 us -> none  [regrouped(): jnp.sum(scaled_out * scaled_out)]
where the time goes in v4:
time: 183 us; the launch traced here: 182 us
  Pallas kernels  144 us (79%)
  matrix products  27.3 us (15%)
  local copies, waits for them, and re-layouts  7.05 us (4%)
    pallas_call x1, Pallas kernels, spread(): pl.pallas_call(functools.partial(spread_kernel, dp, tp, const), out_shape...  82.7 us
    pallas_call x1, Pallas kernels, collect(): pl.pallas_call(functools.partial(collect_kernel, dp, tp), out_shape=(jax....  61.8 us
    dot_general x1, matrix products, regrouped(): jnp.dot(delta, flat_x, preferred_element_type=f32).astype(bf)  9.32 us
    dot_general x1, matrix products, against(): lax.dot_general(weight, tokens, (((0,), (1,)), ((), ())), preferred_eleme...  7.27 us
    dot_general x1, matrix products, regrouped(): yt = jnp.dot(full_out, act, preferred_element_type=f32)  5.92 us
    dot_general x1, matrix products, regrouped(): jnp.dot(act, flat_dy, preferred_element_type=f32).astype(bf)  4.75 us

profile of v4, /device:TPU:0, one launch (start us, length us, event | category | flops | bytes accessed | tf_op | source)
XLA Modules:
  0.0 181.8 jit_solution(969949960767556365)
XLA Ops:
  0.6 82.7 %spread.1 = (bf16[8,160,640]{2,1,0:T(8,128)(2,1)}, bf16[4,4,128,1280]{3,2,1,0:T(8,128)(2,1)}, bf16[4,4,128,1280]{3,2,1,0:T(8,128)(2,1)}, f32[8,128]{1,0:T(8,128)}) custom-call(bf16[160,1280]{1,0:T(8,128)(2,1)} %wi.1, bf16[160,1280]{1,0:T(8,128)(2,1)} %wo.1, f32[160,1280]{1,0:T(8,128)} %gi.1, f32[160,1280]{1,0:T(8,128)} %go.1, ...), custom_call_target="tpu_custom_call" | custom-call | tf_op jit(solution)/shard_map/spread/pallas_call | solution.py:188
  83.3 0.0 copy-start.6
  83.4 7.3 %multiply_convert_fusion = (bf16[320,2048]{1,0:T(8,128)(2,1)}, f32[320,2048]{1,0:T(8,128)}) fusion(bf16[2048,1280]{1,0:T(8,128)(2,1)} %bitcast.29, bf16[1280,640]{1,0:T(8,128)(2,1)} %bitcast.31), kind=kOutput, calls=%fused_computation.10 | convolution fusion | flops 1680998400 | bytes 10158080 | tf_op jit(solution)/shard_map/dot_general | solution.py:344
  90.6 0.0 copy-done.6
  90.6 9.3 %convolution_convert_fusion.2 = bf16[320,1280]{1,0:T(8,128)(2,1)S(1)} fusion(bf16[2048,1280]{1,0:T(8,128)(2,1)} %bitcast.30, bf16[2048,1280]{1,0:T(8,128)(2,1)} %bitcast.27, f32[320,2048]{1,0:T(8,128)} %get-tuple-element.25, bf16[1280,640]{1,0:T(8,128)(2,1)S(1)} %bitcast.33), kind=kOutput, calls=%fused_computation.4 | convolution fusion | flops 3362406400 | bytes 14909440 | tf_op jit(solution)/shard_map/dot_general | solution.py:352
  100.0 4.7 %convolution_convert_fusion.1 = bf16[320,1280]{1,0:T(8,128)(2,1)S(1)} fusion(bf16[320,2048]{1,0:T(8,128)(2,1)} %get-tuple-element.24, bf16[2048,1280]{1,0:T(8,128)(2,1)} %bitcast.28), kind=kOutput, calls=%fused_computation.3 | convolution fusion | flops 1678131200 | bytes 7372800 | tf_op jit(solution)/shard_map/dot_general | solution.py:353
  104.7 0.1 maximum_bitcast_fusion
  104.8 0.0 copy-start.7
  104.8 2.3 %copy.11 = bf16[1280,640]{1,0:T(8,128)(2,1)} copy(bf16[1280,640]{0,1:T(8,128)(2,1)S(1)} %maximum_bitcast_fusion) | data formatting | bytes 3276800 | tf_op jit(solution)/shard_map/transpose | solution.py:354
  107.1 0.0 copy-done.7
  107.1 5.9 %convolution_convert_fusion = bf16[1280,2048]{1,0:T(8,128)(2,1)} fusion(bf16[320,2048]{1,0:T(8,128)(2,1)S(1)} %copy-done.7, bf16[1280,640]{1,0:T(8,128)(2,1)} %bitcast.32), kind=kOutput, calls=%fused_computation | convolution fusion | flops 1680343040 | bytes 7536640 | tf_op jit(solution)/shard_map/dot_general | solution.py:348
  113.0 61.8 %collect.1 = (f32[160,1280]{1,0:T(8,128)}, f32[160,1280]{1,0:T(8,128)}, bf16[320,512]{1,0:T(8,128)(2,1)}) custom-call(bf16[8,160,640]{2,1,0:T(8,128)(2,1)} %bitcast.21, bf16[4,320,2048]{2,1,0:T(8,128)(2,1)} %bitcast.22), custom_call_target="tpu_custom_call" | custom-call | tf_op jit(solution)/shard_map/collect/pallas_call | solution.py:294
  174.8 0.0 copy-start.5
  174.8 1.8 copy.15
  176.6 1.2 slice.11
  178.5 0.0 copy-done
  178.5 0.0 copy-done.1
  178.5 0.0 copy-done.2
  178.5 0.0 copy-done.3
  178.6 0.0 copy-start.4
  178.6 1.4 multiply_multiply_fusion.1
  180.0 0.9 copy.18
  180.9 0.0 copy-done.4
  180.9 0.9 copy.19
  (5 shorter events, 0.0 us)
Async XLA Ops:
  83.3 7.3 %copy-start.6 = (bf16[8,160,640]{2,1,0:T(8,128)(2,1)S(1)}, bf16[8,160,640]{2,1,0:T(8,128)(2,1)}, u32[]{:S(2)}) copy-start(bf16[8,160,640]{2,1,0:T(8,128)(2,1)} %get-tuple-element.12) | copy-start | bytes 4915204
  104.8 2.3 %copy-start.7 = (bf16[320,2048]{1,0:T(8,128)(2,1)S(1)}, bf16[320,2048]{1,0:T(8,128)(2,1)}, u32[]{:S(2)}) copy-start(bf16[320,2048]{1,0:T(8,128)(2,1)} %get-tuple-element.24) | copy-start | bytes 3932164
  113.0 65.5 %copy-start = (f32[160,1280]{1,0:T(8,128)S(1)}, f32[160,1280]{1,0:T(8,128)}, u32[]{:S(2)}) copy-start(f32[160,1280]{1,0:T(8,128)} %gi.1) | copy-start | bytes 2457604
  113.0 65.5 %copy-start.1 = (f32[160,1280]{1,0:T(8,128)S(1)}, f32[160,1280]{1,0:T(8,128)}, u32[]{:S(2)}) copy-start(f32[160,1280]{1,0:T(8,128)} %go.1) | copy-start | bytes 2457604
  113.0 65.5 %copy-start.2 = (bf16[160,1280]{1,0:T(8,128)(2,1)S(1)}, bf16[160,1280]{1,0:T(8,128)(2,1)}, u32[]{:S(2)}) copy-start(bf16[160,1280]{1,0:T(8,128)(2,1)} %wi.1) | copy-start | bytes 1228804
  113.0 65.5 %copy-start.3 = (bf16[160,1280]{1,0:T(8,128)(2,1)S(1)}, bf16[160,1280]{1,0:T(8,128)(2,1)}, u32[]{:S(2)}) copy-start(bf16[160,1280]{1,0:T(8,128)(2,1)} %wo.1) | copy-start | bytes 1228804
  174.8 5.2 %copy-start.5 = (f32[160,1280]{1,0:T(8,128)S(1)}, f32[160,1280]{1,0:T(8,128)}, u32[]{:S(2)}) copy-start(f32[160,1280]{1,0:T(8,128)} %get-tuple-element.36) | copy-start | bytes 2457604
  178.6 2.3 %copy-start.4 = (f32[160,1280]{1,0:T(8,128)S(1)}, f32[160,1280]{1,0:T(8,128)}, u32[]{:S(2)}) copy-start(f32[160,1280]{1,0:T(8,128)} %get-tuple-element.37) | copy-start | bytes 2457604
